TPU v7x, 32 devices: a whole 2x2x4 slice. The times are simulated.
32 devices in a mesh: dp: 4 (over y, x), fsdp: 8 (over z, core).
Axes of the slice: x: 2, y: 2, z: 4, core: 2. Of those that a mesh axis runs over, the one named last changes fastest.
Arguments:
- input_tokens: int32 [2, 32768], P(None, ('dp', 'fsdp')), may hold values from 0 to 29
- item_numbers: int32 [2, 32768], P(None, ('dp', 'fsdp')), may hold values from -1 to 3, as said below
- loss_positions: int32 [2, 4096], P(None, ('dp', 'fsdp')), may hold values from -1 to 1023, as said below
- target_tokens: int32 [2, 4096], P(None, ('dp', 'fsdp')), may hold values from 0 to 29
- input_projection: float32 [1280, 640], P('fsdp', 'dp'), may hold values from -0.15625 to 0.15625
- dilated_conv: float32 [3200, 640], P('fsdp', 'dp'), may hold values from -0.109375 to 0.109375
- output_projection: float32 [1280, 640], P('fsdp', 'dp'), may hold values from -0.25 to 0.25
- vectors: float32 [68, 1280], P(None, ('dp', 'fsdp'))
- input_first_moment: float32 [1280, 640], P('fsdp'), may hold values from -6.67572e-06 to 6.67572e-06
- input_second_moment: float32 [1280, 640], P('fsdp'), may hold values from 5.3002034e-12 to 2.1200814e-11
- conv_first_moment: float32 [3200, 640], P('fsdp'), may hold values from -6.67572e-06 to 6.67572e-06
- conv_second_moment: float32 [3200, 640], P('fsdp'), may hold values from 5.3002034e-12 to 2.1200814e-11
- output_first_moment: float32 [1280, 640], P('fsdp'), may hold values from -6.67572e-06 to 6.67572e-06
- output_second_moment: float32 [1280, 640], P('fsdp'), may hold values from 5.3002034e-12 to 2.1200814e-11
- vector_first_moment: float32 [68, 1280], P(None, ('dp', 'fsdp')), may hold values from -1.9073486e-05 to 1.9073486e-05
- vector_second_moment: float32 [68, 1280], P(None, ('dp', 'fsdp')), may hold values from 4.7701832e-11 to 1.9080733e-10
- bases: float32 [3, 640, 640], replicated, as said below
- eigenbasis_flags: int32 [3], replicated, may hold values from 0 to 1, as said below
- optimizer_step: int32 [1], replicated, may hold values from 2 to 20
Outputs:
- mean_loss: float32 [], replicated
- grad_norm: float32 [], replicated
- master_in: float32 [1280, 640], P('fsdp', 'dp')
- copy_in: bfloat16 [1280, 640], P('fsdp', 'dp')
- moment_in: float32 [1280, 640], P('fsdp')
- square_in: float32 [1280, 640], P('fsdp')
- updated_conv: float32 [3200, 640], P('fsdp', 'dp')
- conv_bfloat_copy: bfloat16 [3200, 640], P('fsdp', 'dp')
- updated_conv_moment: float32 [3200, 640], P('fsdp')
- updated_conv_square: float32 [3200, 640], P('fsdp')
- master_out: float32 [1280, 640], P('fsdp', 'dp')
- copy_out: bfloat16 [1280, 640], P('fsdp', 'dp')
- moment_out: float32 [1280, 640], P('fsdp')
- square_out: float32 [1280, 640], P('fsdp')
- master_vec: float32 [68, 1280], P(None, ('dp', 'fsdp'))
- copy_vec: bfloat16 [68, 1280], P(None, ('dp', 'fsdp'))
- moment_vec: float32 [68, 1280], P(None, ('dp', 'fsdp'))
- square_vec: float32 [68, 1280], P(None, ('dp', 'fsdp'))
Inputs may be any that keep to these rules, and one draw needn't show every extreme that they name: `item_numbers`: each device's 1024 slots of a micro-batch hold whole items of 256, 512 or 1024 tokens, numbered from 0 in order and starting at slot 0, followed by padding marked -1; items fill at least half of the slots; some device holds one item of 1024 tokens. `loss_positions`: slot i of a device's 128 slots in a micro-batch holds -1 or a position from 8 i to 8 i + 7 of that device's slots; it holds a position exactly when that position belongs to an item. `eigenbasis_flags`: two of the three entries are 1. `bases`: each matrix is orthogonal.
All inputs are finite; a program needn't handle non-finite values.
Results may differ from a plain program's by a relative error of at most 0.0091.
Values may be sent and summed in bfloat16 or wider, within the bound.
A program may use at most 256 MiB of HBM per device.

v0:
```python
from functools import partial
import jax
import jax.numpy as jnp
from jax import lax
from jax.sharding import PartitionSpec as P

VOCAB = 30
CONV_TAPS = 5
DILATION = 8
TABLE = 32
beta_one = 0.9
beta_two = 0.95
epsilon = 1e-08
rate_matrix = 0.02
rate_vector = 0.5
decay_weight = 0.01
clip_limit = 0.02
norm_eps = 1e-05
highest_precision = lax.Precision.HIGHEST


def layer_norm(values, norm_gain, norm_bias):
    centre = values - jnp.mean(values, axis=-1, keepdims=True)
    spread = jnp.mean(centre * centre, axis=-1, keepdims=True)
    return centre * lax.rsqrt(spread + norm_eps) * norm_gain + norm_bias


def norm_gelu(values, norm_gain, norm_bias):
    return jax.nn.gelu(layer_norm(values, norm_gain, norm_bias), approximate=True)


def slot_loss(logits, labels, valid_slot):
    log_total = jax.nn.logsumexp(logits, axis=-1)
    hits = labels[:, None] == jnp.arange(logits.shape[1], dtype=jnp.int32)[None, :]
    chosen = jnp.sum(jnp.where(hits, logits, 0.0), axis=-1)
    return jnp.sum(jnp.where(valid_slot, log_total - chosen, 0.0))


def moved_groups(values, step):
    if step > 0:
        return jnp.concatenate([values[:, step:], jnp.full_like(values[:, :step], -1)], axis=1)
    if step < 0:
        return jnp.concatenate([jnp.full_like(values[:, :-step], -1), values[:, :step]], axis=1)
    return values


def tap_onehots(tokens, items, positions):
    batches, slots = positions.shape
    stride = tokens.shape[1] // slots
    token_groups = tokens.reshape(batches, slots, stride)
    item_groups = items.reshape(batches, slots, stride)
    valid = positions >= 0
    residue = jnp.where(valid, positions - stride * jnp.arange(slots, dtype=jnp.int32)[None], -1)
    chosen = residue[:, :, None] == jnp.arange(stride, dtype=jnp.int32)[None, None]
    own_item = jnp.sum(jnp.where(chosen, item_groups, 0), axis=2)
    identities = jnp.arange(TABLE, dtype=jnp.int32)
    result = []
    for tap in range(CONV_TAPS):
        step = (tap - CONV_TAPS // 2) * DILATION // stride
        item = jnp.sum(jnp.where(chosen, moved_groups(item_groups, step), 0), axis=2)
        token = jnp.sum(jnp.where(chosen, moved_groups(token_groups, step), 0), axis=2)
        keep = valid & (item == own_item) & (own_item >= 0)
        result.append(jnp.where(keep, token, -1)[:, :, None] == identities)
    return jnp.concatenate(result, axis=2).reshape(batches * slots, CONV_TAPS * TABLE)


def exact_dot(left, right, contract):
    high = left.astype(jnp.bfloat16)
    low = (left - high.astype(jnp.float32)).astype(jnp.bfloat16)
    return lax.dot_general(
        high, right, contract, preferred_element_type=jnp.float32
    ) + lax.dot_general(low, right, contract, preferred_element_type=jnp.float32)


def column_sum(values):
    return jnp.sum(values, axis=0, dtype=jnp.float32)


def gathered_weights(shards):
    parted = (
        lax.all_gather(shards[0], "fsdp", axis=0, tiled=True),
        lax.all_gather(shards[1], "fsdp", axis=0, tiled=True),
        lax.all_gather(shards[2], "fsdp", axis=0, tiled=True),
        lax.all_gather(shards[3], "fsdp", axis=1, tiled=True),
    )
    return (
        lax.all_gather(parted[0], "dp", axis=1, tiled=True),
        lax.all_gather(parted[1], "dp", axis=1, tiled=True),
        lax.all_gather(parted[2], "dp", axis=1, tiled=True),
        lax.all_gather(parted[3], "dp", axis=1, tiled=True),
    )


def eigenbasis_update(
    gradient, master, moment, square, rotated_grads, col_start, first_correction, second_correction
):
    rotated = jnp.dot(gradient, rotated_grads, precision=highest_precision)
    moment_new = beta_one * moment + (1.0 - beta_one) * rotated
    square_new = beta_two * square + (1.0 - beta_two) * rotated * rotated
    step_ratio = (
        moment_new / first_correction / (jnp.sqrt(square_new / second_correction) + epsilon)
    )
    own_basis = lax.dynamic_slice_in_dim(rotated_grads, col_start, master.shape[1], 0)
    update = jnp.einsum("ri,ci->rc", step_ratio, own_basis, precision=highest_precision)
    master_new = master - rate_matrix * (update + decay_weight * master)
    return (master_new, master_new.astype(jnp.bfloat16), moment_new, square_new)


def adam_vectors(gradient, master, moment, square, first_correction, second_correction):
    decay_rows = jnp.where(
        jnp.arange(master.shape[0], dtype=jnp.int32)[:, None] < 2 * VOCAB, decay_weight, 0.0
    )
    moment_new = beta_one * moment + (1.0 - beta_one) * gradient
    square_new = beta_two * square + (1.0 - beta_two) * gradient * gradient
    step_ratio = (
        moment_new / first_correction / (jnp.sqrt(square_new / second_correction) + epsilon)
    )
    master_new = master - rate_vector * (step_ratio + decay_rows * master)
    return (master_new, master_new.astype(jnp.bfloat16), moment_new, square_new)


def local(
    input_tokens,
    item_numbers,
    loss_positions,
    target_tokens,
    input_projection,
    dilated_conv,
    output_projection,
    vectors,
    input_first_moment,
    input_second_moment,
    conv_first_moment,
    conv_second_moment,
    output_first_moment,
    output_second_moment,
    vector_first_moment,
    vector_second_moment,
    bases,
    eigenbasis_flags,
    optimizer_step,
):
    shards_low = (
        input_projection.astype(jnp.bfloat16),
        dilated_conv.astype(jnp.bfloat16),
        output_projection.astype(jnp.bfloat16),
        vectors.astype(jnp.bfloat16),
    )
    weight_in, weight_conv, weight_out, table_low = gathered_weights(shards_low)
    groups, col_index = (lax.axis_size("dp"), lax.axis_index("dp"))
    rows, row_index = (lax.axis_size("fsdp"), lax.axis_index("fsdp"))
    inner = weight_in.shape[1]
    width = weight_in.shape[0]
    start = 2 * VOCAB
    table = table_low.astype(jnp.float32)
    head = table_low[VOCAB:start]
    onehots = tap_onehots(input_tokens, item_numbers, loss_positions)
    onehots_low = onehots.astype(jnp.bfloat16)
    centre = CONV_TAPS // 2 * TABLE
    centre_low = onehots_low[:, centre : centre + TABLE]
    embedded = jnp.concatenate(
        [table_low[:VOCAB], jnp.zeros((TABLE - VOCAB, width), jnp.bfloat16)], axis=0
    )
    first_act, first_back = jax.vjp(
        norm_gelu, embedded.astype(jnp.float32), table[start], table[start + 1]
    )
    first_low = first_act.astype(jnp.bfloat16)
    pre_inner = (
        jnp.dot(first_low, weight_in, preferred_element_type=jnp.float32) + table[start + 6, :inner]
    )
    second_act, second_back = jax.vjp(
        norm_gelu, pre_inner, table[start + 5, :inner], table[start + 5, inner:]
    )
    second_low = second_act.astype(jnp.bfloat16)
    picked_act = [
        jnp.dot(
            onehots_low[:, tap * TABLE : (tap + 1) * TABLE],
            second_low,
            preferred_element_type=jnp.float32,
        ).astype(jnp.bfloat16)
        for tap in range(CONV_TAPS)
    ]
    conv_input = (
        jnp.dot(
            jnp.concatenate(picked_act, axis=1), weight_conv, preferred_element_type=jnp.float32
        )
        + table[start + 6, inner:]
    )
    third_act, third_back = jax.vjp(
        norm_gelu, conv_input, table[start + 7, :inner], table[start + 7, inner:]
    )
    third_low = third_act.astype(jnp.bfloat16)
    branch = (
        jnp.einsum("ti,di->td", third_low, weight_out, preferred_element_type=jnp.float32)
        + table[start + 2]
    )
    picked_embedded = jnp.dot(centre_low, embedded, preferred_element_type=jnp.float32)
    final_out, final_back = jax.vjp(
        layer_norm, picked_embedded + branch, table[start + 3], table[start + 4]
    )
    picked = final_out.astype(jnp.bfloat16)
    logits = jnp.einsum("pd,vd->pv", picked, head, preferred_element_type=jnp.float32)
    valid = loss_positions.reshape(-1) >= 0
    summed_loss, loss_back = jax.vjp(
        partial(slot_loss, labels=target_tokens.reshape(-1), valid_slot=valid), logits
    )
    logit_grad = loss_back(jnp.ones((), jnp.float32))[0].astype(jnp.bfloat16)
    head_grad = jnp.einsum("pv,pd->vd", logit_grad, picked, preferred_element_type=jnp.float32)
    picked_grad = jnp.dot(logit_grad, head, preferred_element_type=jnp.float32)
    sum_grad, gain_four, bias_four = final_back(picked_grad)
    branch_low = sum_grad.astype(jnp.bfloat16)
    out_grad = jnp.einsum("td,ti->di", branch_low, third_low, preferred_element_type=jnp.float32)
    third_grad = jnp.dot(branch_low, weight_out, preferred_element_type=jnp.float32)
    conv_pre, gain_three, bias_three = third_back(third_grad)
    conv_low = conv_pre.astype(jnp.bfloat16)
    tap_grads = lax.dot_general(
        onehots_low, conv_low, (((0,), (0,)), ((), ())), preferred_element_type=jnp.float32
    )
    start_grads = jnp.einsum(
        "tv,td->vd", centre_low.astype(jnp.float32), sum_grad, precision=highest_precision
    )
    slot_count = jnp.sum(valid.astype(jnp.float32))
    wide_rows = jnp.concatenate(
        [
            start_grads[:VOCAB],
            head_grad,
            jnp.stack(
                [
                    column_sum(branch_low),
                    gain_four,
                    bias_four,
                    jnp.concatenate([gain_three, bias_three]),
                ]
            ),
        ],
        axis=0,
    )
    out_rows = lax.psum(
        lax.psum_scatter(out_grad.astype(jnp.bfloat16), "fsdp", scatter_dimension=0, tiled=True),
        "dp",
    ).astype(jnp.float32)
    tap_grads, wide_rows, summed_loss, slot_count = lax.psum(
        (tap_grads, wide_rows, summed_loss, slot_count), ("dp", "fsdp")
    )
    tap_view = tap_grads.reshape(CONV_TAPS, TABLE, inner)
    second_grad = sum(
        (
            exact_dot(
                tap_view[tap],
                weight_conv[tap * inner : (tap + 1) * inner],
                (((1,), (1,)), ((), ())),
            )
            for tap in range(CONV_TAPS)
        )
    )
    inner_pre, gain_two, bias_two = second_back(second_grad)
    first_grad = exact_dot(inner_pre, weight_in, (((1,), (1,)), ((), ())))
    table_grad, gain_one, bias_one = first_back(first_grad)
    vec_sum = jnp.concatenate(
        [
            table_grad[:VOCAB] + wide_rows[:VOCAB],
            wide_rows[VOCAB:start],
            jnp.stack(
                [
                    gain_one,
                    bias_one,
                    wide_rows[start],
                    wide_rows[start + 1],
                    wide_rows[start + 2],
                    jnp.concatenate([gain_two, bias_two]),
                    jnp.concatenate(
                        [jnp.sum(inner_pre, axis=0), jnp.sum(tap_view[CONV_TAPS // 2], axis=0)]
                    ),
                    wide_rows[start + 3],
                ]
            ),
        ],
        axis=0,
    )
    own = width // (groups * rows)
    vec_own = lax.dynamic_slice_in_dim(vec_sum, (col_index * rows + row_index) * own, own, 1)
    row_low = lax.dynamic_slice_in_dim(first_low, row_index * (width // rows), width // rows, 1)
    in_rows = jnp.einsum(
        "vr,vi->ri", row_low.astype(jnp.float32), inner_pre, precision=highest_precision
    )
    placed = (
        jnp.eye(CONV_TAPS, dtype=jnp.bfloat16)[:, None, :, None] * second_low[None, :, None, :]
    ).reshape(CONV_TAPS * TABLE, CONV_TAPS * inner)
    conv_count = CONV_TAPS * inner // rows
    conv_low_rows = lax.dynamic_slice_in_dim(placed, row_index * conv_count, conv_count, 1)
    conv_rows = jnp.einsum(
        "vr,vi->ri", conv_low_rows.astype(jnp.float32), tap_grads, precision=highest_precision
    )
    col_width = input_projection.shape[1]
    col_start = col_index * col_width
    owned = [
        lax.dynamic_slice_in_dim(full_rows, col_start, col_width, 1)
        for full_rows in (in_rows, conv_rows, out_rows)
    ]
    square_local = sum((jnp.sum(piece * piece) for piece in owned)) + jnp.sum(vec_own * vec_own)
    square_total = lax.psum(square_local, ("dp", "fsdp"))
    grad_norm = jnp.sqrt(square_total) / slot_count
    factor = jnp.minimum(1.0, clip_limit / grad_norm) / slot_count
    step_value = optimizer_step[0].astype(jnp.float32)
    first_correction = 1.0 - beta_one**step_value
    second_correction = 1.0 - beta_two**step_value
    identity = jnp.eye(bases.shape[1], dtype=jnp.float32)
    rotated_grads = [
        jnp.where(eigenbasis_flags[mat_index] == 1, bases[mat_index], identity)
        for mat_index in range(3)
    ]
    master_in, copy_in, moment_in, square_in = eigenbasis_update(
        in_rows * factor,
        input_projection,
        input_first_moment,
        input_second_moment,
        rotated_grads[0],
        col_start,
        first_correction,
        second_correction,
    )
    updated_conv, conv_bfloat_copy, updated_conv_moment, updated_conv_square = eigenbasis_update(
        conv_rows * factor,
        dilated_conv,
        conv_first_moment,
        conv_second_moment,
        rotated_grads[1],
        col_start,
        first_correction,
        second_correction,
    )
    master_out, copy_out, moment_out, square_out = eigenbasis_update(
        out_rows * factor,
        output_projection,
        output_first_moment,
        output_second_moment,
        rotated_grads[2],
        col_start,
        first_correction,
        second_correction,
    )
    master_vec, copy_vec, moment_vec, square_vec = adam_vectors(
        vec_own * factor,
        vectors,
        vector_first_moment,
        vector_second_moment,
        first_correction,
        second_correction,
    )
    return (
        summed_loss / slot_count,
        grad_norm,
        master_in,
        copy_in,
        moment_in,
        square_in,
        updated_conv,
        conv_bfloat_copy,
        updated_conv_moment,
        updated_conv_square,
        master_out,
        copy_out,
        moment_out,
        square_out,
        master_vec,
        copy_vec,
        moment_vec,
        square_vec,
    )


def solution(mesh):
    placed = (
        P(None, ("dp", "fsdp")),
        P(None, ("dp", "fsdp")),
        P(None, ("dp", "fsdp")),
        P(None, ("dp", "fsdp")),
        P("fsdp", "dp"),
        P("fsdp", "dp"),
        P("fsdp", "dp"),
        P(None, ("dp", "fsdp")),
        P("fsdp", None),
        P("fsdp", None),
        P("fsdp", None),
        P("fsdp", None),
        P("fsdp", None),
        P("fsdp", None),
        P(None, ("dp", "fsdp")),
        P(None, ("dp", "fsdp")),
        P(),
        P(),
        P(),
    )
    return jax.shard_map(
        local,
        mesh=mesh,
        in_specs=placed,
        out_specs=(
            P(),
            P(),
            P("fsdp", "dp"),
            P("fsdp", "dp"),
            P("fsdp", None),
            P("fsdp", None),
            P("fsdp", "dp"),
            P("fsdp", "dp"),
            P("fsdp", None),
            P("fsdp", None),
            P("fsdp", "dp"),
            P("fsdp", "dp"),
            P("fsdp", None),
            P("fsdp", None),
            P(None, ("dp", "fsdp")),
            P(None, ("dp", "fsdp")),
            P(None, ("dp", "fsdp")),
            P(None, ("dp", "fsdp")),
        ),
        check_vma=False,
    )
```

profile of v0, /device:TPU:0, one launch (start us, length us, event | category | flops | bytes accessed | tf_op | source)
XLA Modules:
  0.0 448.6 jit_solution(13318790857752670244)
XLA Ops:
  8.2 17.0 %all_gather.26 = bf16[1280,160]{1,0:T(8,128)(2,1)S(1)} all-gather(bf16[160,160]{1,0:T(8,128)(2,1)S(1)} %convert_element_type.159), channel_id=1, replica_groups=mesh['dp'=4,'fsdp'=8] {'fsdp'}, dimensions={0}, use_global_device_ids=true | all-gather | bytes 460800 | tf_op jit(solution)/shard_map/all_gather | solution.py:81
  26.2 19.0 %all-gather.1 = bf16[8,400,160]{1,2,0:T(8,128)(2,1)S(1)} all-gather(bf16[1,400,160]{1,2,0:T(8,128)(2,1)S(1)} %convert_bitcast_fusion), channel_id=1, replica_groups=mesh['dp'=4,'fsdp'=8] {'fsdp'}, dimensions={0}, use_global_device_ids=true | all-gather | bytes 1152000 | tf_op jit(solution)/shard_map/all_gather | solution.py:82
  46.0 2.4 reshape.268
  48.5 15.1 %all_gather.30 = bf16[1280,160]{1,0:T(8,128)(2,1)S(1)} all-gather(bf16[160,160]{1,0:T(8,128)(2,1)S(1)} %convert_element_type.168), channel_id=1, replica_groups=mesh['dp'=4,'fsdp'=8] {'fsdp'}, dimensions={0}, use_global_device_ids=true | all-gather | bytes 460800 | tf_op jit(solution)/shard_map/all_gather | solution.py:83
  65.4 13.9 %all_gather.24 = bf16[68,320]{0,1:T(8,128)(2,1)S(1)} all-gather(bf16[68,40]{0,1:T(8,128)(2,1)S(1)} %convert_element_type.155), channel_id=1, replica_groups=mesh['dp'=4,'fsdp'=8] {'fsdp'}, dimensions={1}, use_global_device_ids=true | all-gather | bytes 48960 | tf_op jit(solution)/shard_map/all_gather | solution.py:84
  79.4 9.3 %all-gather = bf16[4,320,68]{1,2,0:T(8,128)(2,1)S(1)} all-gather(bf16[1,320,68]{1,2,0:T(8,128)(2,1)S(1)} %copy.91), channel_id=1, replica_groups=mesh['dp'=4,'fsdp'=8] {'dp'}, dimensions={0}, use_global_device_ids=true | all-gather | bytes 217600 | tf_op jit(solution)/shard_map/all_gather | solution.py:90
  89.0 1.8 slice_reduce_fusion.1
  90.9 1.1 slice_reduce_fusion.6
  98.2 4.6 %convert_select_fusion = (f32[640,640]{1,0:T(8,128)}, f32[640,640]{1,0:T(8,128)}, f32[640,640]{1,0:T(8,128)S(1)}) fusion(f32[3,640,640]{2,1,0:T(8,128)} %param.35, pred[]{:T(512)} %bitcast.22, pred[]{:T(512)} %bitcast.16, pred[]{:T(512)} %bitcast.20), kind=kLoop, calls=%fused_computation.1 | loop fusion | flops 2048000 | bytes 9830403 | tf_op jit(solution)/shard_map/jit(_where)/select_n | solution.py:309
  103.1 2.2 fusion.164
  105.8 1.1 copy.112
  108.0 1.1 fusion.5
  111.2 1.1 fusion.2
  112.9 4.3 fusion.165
  117.4 29.3 %all-gather.10.cloned.1.call-done = bf16[1280,640]{0,1:T(8,128)(2,1)} async-done(((bf16[1280,160]{0,1:T(8,128)(2,1)}), bf16[1280,640]{0,1:T(8,128)(2,1)}) %all-gather.10.cloned.1.call-update) | async-done | bytes 1638416 | tf_op jit(solution)/shard_map/all_gather | solution.py:89
  146.8 2.3 convolution_add_fusion.1
  152.7 1.5 fusion
  154.4 1.1 multiply_reduce_fusion.3
  155.5 1.1 stack.21
  156.6 1.1 stack.20
  158.8 1.1 reshape.270
  160.3 1.1 fusion.91
  161.3 4.6 %concatenate.62 = f32[64,1280]{0,1:T(8,128)} concatenate(f32[30,1280]{0,1:T(8,128)S(1)} %fusion, f32[30,1280]{0,1:T(8,128)S(1)} %fusion.150, f32[1,1280]{0,1:T(8,128)} %stack.20, f32[1,1280]{0,1:T(8,128)} %reshape.269, f32[1,1280]{0,1:T(8,128)} %reshape.270, f32[1,1280]{0,1:T(8,128)} %stack.21), dimensions={0} | concatenate | bytes 655360 | tf_op jit(solution)/shard_map/concatenate | solution.py:223
  166.6 3.4 convolution_convert_fusion
  170.1 126.9 %all-reduce.15.cloned.1.call-done = (f32[160,640]{1,0:T(8,128)}, f32[64,1280]{0,1:T(8,128)}) async-done(((f32[160,640]{1,0:T(8,128)}, f32[64,1280]{0,1:T(8,128)}), (f32[160,640]{1,0:T(8,128)}, f32[64,1280]{0,1:T(8,128)})) %all-reduce.15.cloned.1.call-update) | async-done | bytes 737296 | tf_op jit(solution)/shard_map/psum | solution.py:242
  296.9 2.3 slice.225
  299.2 2.2 slice.226
  301.4 1.4 fusion.32
  302.8 1.4 fusion.35
  306.9 1.1 stack.23
  308.0 1.1 stack.22
  309.9 1.8 fusion.55
  312.7 1.1 reshape.272
  313.9 1.1 fusion.117
  316.1 1.3 fusion.158
  317.3 16.7 %reduce-scatter.2.cloned.1.call-done = bf16[160,640]{1,0:T(8,128)(2,1)} async-done(((bf16[1280,640]{1,0:T(8,128)(2,1)}), bf16[160,640]{1,0:T(8,128)(2,1)}) %reduce-scatter.2.cloned.1.call-update) | async-done | bytes 204816 | tf_op jit(solution)/shard_map/reduce_scatter | solution.py:239
  334.1 1.7 fusion.105
  337.9 4.8 %concatenate.65 = f32[68,1280]{0,1:T(8,128)} concatenate(f32[30,1280]{0,1:T(8,128)} %get-tuple-element.155, f32[30,1280]{0,1:T(8,128)} %get-tuple-element.154, f32[1,1280]{0,1:T(8,128)} %reshape.271, f32[1,1280]{0,1:T(8,128)} %reshape.272, f32[3,1280]{0,1:T(8,128)} %slice.225, f32[1,1280]{0,1:T(8,128)} %stack.22, f32[1,1280]{0,1:T(8,128)} %stack.23, f32[1,1280]{0,1:T(8,128)} %slice.226), dimensions={0} | concatenate | bytes 696320 | tf_op jit(solution)/shard_map/concatenate | solution.py:259
  342.7 1.3 multiply_reduce_fusion.12
  344.0 33.6 %all-reduce.13.cloned.1.call-done = bf16[160,640]{1,0:T(8,128)(2,1)} async-done(((bf16[160,640]{1,0:T(8,128)(2,1)}), bf16[160,640]{1,0:T(8,128)(2,1)}) %all-reduce.13.cloned.1.call-update) | async-done | bytes 204816 | tf_op jit(solution)/shard_map/psum | solution.py:238
  380.6 40.0 %all-reduce.8 = (f32[]{:T(128)}, f32[]{:T(128)}, f32[]{:T(128)}) all-reduce(f32[]{:T(128)} %get-tuple-element.126, f32[]{:T(128)} %get-tuple-element.125, f32[]{:T(128)S(6)} %add.335), channel_id=1, replica_groups=mesh['dp'=4,'fsdp'=8] {'dp','fsdp'}, use_global_device_ids=true, to_apply=%region_22.23 | all-reduce | flops 3 | bytes 24 | tf_op jit(solution)/shard_map/psum | solution.py:242
  424.7 4.8 %fusion.17 = (f32[400,640]{1,0:T(8,128)S(1)}, f32[400,640]{1,0:T(8,128)S(1)}) fusion(f32[400,640]{1,0:T(8,128)} %param.30, f32[400,640]{1,0:T(8,128)} %param.29, f32[640,640]{1,0:T(8,128)S(1)} %get-tuple-element.151, f32[400,640]{1,0:T(8,128)S(1)} %fusion.105, f32[]{:T(128)S(6)} %div.159), kind=kOutput, calls=%fused_computation.48 | convolution fusion | flops 1968128000 | bytes 6758404 | tf_op jit(solution)/shard_map/dot_general | solution.py:97
  429.6 1.4 fusion.73
  431.0 1.4 fusion.170
  432.5 2.4 fusion.169
  434.9 1.4 fusion.72
  436.4 1.4 fusion.168
  437.9 1.4 fusion.151
  (193 shorter events, 27.0 us)
Async XLA Ops:
  7.2 19.0 %copy-start.23 = (f32[400,160]{0,1:T(8,128)S(1)}, f32[400,160]{0,1:T(8,128)}, u32[]{:S(2)}) copy-start(f32[400,160]{0,1:T(8,128)} %param.24) | copy-start | bytes 768004
  7.2 95.8 %all-gather.6.cloned.1.call-start = ((), (), s32[]{:S(2)}) async-start(), calls=%async_computation.1 | async-start | bytes 2048000 | tf_op jit(solution)/shard_map/all_gather | solution.py:87
  26.2 86.8 %all-gather.8.cloned.1.call-start = ((), (), s32[]{:S(2)}) async-start(), calls=%async_computation.2 | async-start | bytes 5120000 | tf_op jit(solution)/shard_map/all_gather | solution.py:88
  46.0 2.5 copy-start.25
  48.4 16.3 %copy-start.33 = (s32[2,1024]{1,0:T(2,128)S(1)}, s32[2,1024]{1,0:T(2,128)}, u32[]{:S(2)}) copy-start(s32[2,1024]{1,0:T(2,128)} %param.20) | copy-start | bytes 24580
  48.4 16.4 %copy-start.34 = (s32[2,1024]{1,0:T(2,128)S(1)}, s32[2,1024]{1,0:T(2,128)}, u32[]{:S(2)}) copy-start(s32[2,1024]{1,0:T(2,128)} %param.19) | copy-start | bytes 24580
  48.5 98.3 %all-gather.10.cloned.1.call-start = ((), (), s32[]{:S(2)}) async-start(), calls=%async_computation.3 | async-start | bytes 2048000 | tf_op jit(solution)/shard_map/all_gather | solution.py:89
  64.6 232.3 %all-reduce.15.cloned.1.call-start = ((), (), s32[]{:S(2)}) async-start(), calls=%async_computation.6 | async-start | bytes 2129920 | tf_op jit(solution)/shard_map/psum | solution.py:242
  90.8 1.7 copy-start.36
  90.8 1.7 copy-start.31
  90.8 4.4 copy-start.35
  98.2 4.8 %copy-start.10 = (bf16[32,1280]{0,1:T(8,128)(2,1)}, bf16[32,1280]{0,1:T(8,128)(2,1)S(1)}, u32[]{:S(2)}) copy-start(bf16[32,1280]{0,1:T(8,128)(2,1)S(1)} %fusion.52) | copy-start | bytes 245764
  105.4 1.5 copy-start.42
  105.4 1.5 copy-start.37
  117.2 31.9 %copy-start.6 = (f32[256,640]{1,0:T(8,128)}, f32[256,640]{1,0:T(8,128)S(1)}, u32[]{:S(2)}) copy-start(f32[256,640]{1,0:T(8,128)S(1)} %get-tuple-element.179) | copy-start | bytes 1966084
  149.9 0.9 copy-start.32
  152.5 1.7 copy-start.7
  152.5 1.9 copy-start.44
  152.7 2.8 copy-start.14
  165.9 168.1 %reduce-scatter.2.cloned.1.call-start = ((), (), s32[]{:S(2)}) async-start(), calls=%async_computation.4 | async-start | bytes 1843200 | tf_op jit(solution)/shard_map/reduce_scatter | solution.py:239
  170.0 207.6 %all-reduce.13.cloned.1.call-start = ((), (), s32[]{:S(2)}) async-start(), calls=%async_computation.5 | async-start | bytes 409600 | tf_op jit(solution)/shard_map/psum | solution.py:238
  296.9 4.5 copy-start.5
  296.9 7.3 %copy-start = (bf16[3200,640]{0,1:T(8,128)(2,1)S(1)}, bf16[3200,640]{0,1:T(8,128)(2,1)}, u32[]{:S(2)}) copy-start(bf16[3200,640]{0,1:T(8,128)(2,1)} %all-gather.8.cloned.1.call-done) | copy-start | bytes 12288004
  305.3 0.8 copy-start.38
  306.1 3.0 copy-start.2
  311.6 4.1 copy-start.41
  312.7 3.3 copy-start.1
  315.0 0.8 copy-start.8
  424.6 4.9 %copy-start.3 = (f32[640,640]{1,0:T(8,128)S(1)}, f32[640,640]{1,0:T(8,128)}, u32[]{:S(2)}) copy-start(f32[640,640]{1,0:T(8,128)} %get-tuple-element.149) | copy-start | bytes 4915204
  424.6 4.9 %copy-start.13 = (bf16[160,640]{1,0:T(8,128)(2,1)S(1)}, bf16[160,640]{1,0:T(8,128)(2,1)}, u32[]{:S(2)}) copy-start(bf16[160,640]{1,0:T(8,128)(2,1)} %all-reduce.13.cloned.1.call-done) | copy-start | bytes 614404
  424.7 4.9 %copy-start.15 = (f32[160,640]{1,0:T(8,128)S(1)}, f32[160,640]{1,0:T(8,128)}, u32[]{:S(2)}) copy-start(f32[160,640]{1,0:T(8,128)} %param.32) | copy-start | bytes 1228804
  424.7 4.9 %copy-start.16 = (f32[160,640]{1,0:T(8,128)S(1)}, f32[160,640]{1,0:T(8,128)}, u32[]{:S(2)}) copy-start(f32[160,640]{1,0:T(8,128)} %param.31) | copy-start | bytes 1228804
  429.5 3.0 copy-start.11
  429.5 3.0 copy-start.12
  429.5 1.5 copy-start.26
  431.0 1.5 copy-start.19
  431.0 1.5 copy-start.20
  431.0 1.4 copy-start.24
  432.5 2.4 copy-start.4
  432.5 2.4 copy-start.9
  432.5 2.4 copy-start.17
  432.5 2.4 copy-start.18
  434.9 1.4 copy-start.27
  436.3 1.5 copy-start.21
  436.4 1.5 copy-start.22
  436.4 1.5 copy-start.29
  436.4 1.5 copy-start.30
  436.4 1.5 copy-start.39
  (3 other events, 2.0 us)
Sparse Core Ops, SparseCore 0:
  26.3 32.3 all-gather.5
  61.1 51.7 all-gather.7
  115.3 31.3 all-gather.9
  166.0 130.8 all-reduce.14
  299.1 34.9 reduce-scatter.1
  336.9 40.6 all-reduce.12
where the time goes:
time: 454 us; the launch traced here: 449 us
  waiting for transfers between devices  207 us (46%)
  blocking collectives  114 us (25%)
  matrix products  46.6 us (10%)
  local copies, waits for them, and re-layouts  34.3 us (8%)
  between operations  27 us (6%)
  other arithmetic  18.8 us (4%)
    psum x1, waiting for transfers between devices, local(): lax.psum((tap_grads, wide_rows, summed_loss, slot_count), ('dp', 'fsdp'))  127 us
    psum x1, blocking collectives, local(): lax.psum((tap_grads, wide_rows, summed_loss, slot_count), ('dp', 'fsdp'))  40 us
    psum x1, waiting for transfers between devices, local(): lax.psum(lax.psum_scatter(out_grad.astype(jnp.bfloat16), 'fsdp', scatter_...  33.6 us
    all_gather x1, waiting for transfers between devices, gathered_weights(): lax.all_gather(parted[2], 'dp', axis=1, tiled=True)  29.3 us
    all_gather x1, blocking collectives, gathered_weights(): lax.all_gather(shards[1], 'fsdp', axis=0, tiled=True)  19 us
    all_gather x1, blocking collectives, gathered_weights(): lax.all_gather(shards[0], 'fsdp', axis=0, tiled=True)  17 us
    reduce_scatter x1, waiting for transfers between devices, local(): lax.psum_scatter(out_grad.astype(jnp.bfloat16), 'fsdp', scatter_dimension...  16.7 us
    all_gather x1, blocking collectives, gathered_weights(): lax.all_gather(shards[2], 'fsdp', axis=0, tiled=True)  15.1 us
  transfers between devices with their start and end apart: 6, of which 5 were waited for; matrix products, arithmetic and copies ran while one was open for 14% of the time, Pallas kernels for 0%

commit v1 on v0

--- a/solution.py
+++ b/solution.py
@@ -235,9 +235,14 @@
         ],
         axis=0,
     )
-    out_rows = lax.psum(
-        lax.psum_scatter(out_grad.astype(jnp.bfloat16), "fsdp", scatter_dimension=0, tiled=True),
-        "dp",
+    out_rows = jnp.sum(
+        lax.all_gather(
+            lax.psum_scatter(
+                out_grad.astype(jnp.bfloat16), "fsdp", scatter_dimension=0, tiled=True
+            ),
+            "dp",
+        ),
+        axis=0,
     ).astype(jnp.float32)
     tap_grads, wide_rows, summed_loss, slot_count = lax.psum(
         (tap_grads, wide_rows, summed_loss, slot_count), ("dp", "fsdp")

time: 454 us -> 421 us (0.927)
  waiting for transfers between devices: 207 us -> 163 us
  blocking collectives: 114 us -> 124 us
    psum x1 -> x0, waiting for transfers between devices: 33.6 us -> none  [local(): lax.psum(lax.psum_scatter(out_grad.astype(jnp.bfloat16), 'fsdp', scatter_...]
    all_gather x0 -> x1, blocking collectives: none -> 12.4 us  [local(): lax.all_gather(lax.psum_scatter(out_grad.astype(jnp.bfloat16), 'fsdp', sc...]
    reduce_scatter x1, waiting for transfers between devices: 16.7 us -> 5.59 us  [local(): lax.psum_scatter(out_grad.astype(jnp.bfloat16), 'fsdp', scatter_dimension...]
  transfers between devices with their start and end apart: 6 -> 5, of which waited for: 5 -> 4; matrix products, arithmetic and copies ran while one was open for 14% -> 15% of each run, Pallas kernels for 0% -> 0%
where the time goes in v1:
time: 421 us; the launch traced here: 415 us
  waiting for transfers between devices  163 us (39%)
  blocking collectives  124 us (29%)
  matrix products  48.6 us (12%)
  local copies, waits for them, and re-layouts  34.2 us (8%)
  between operations  26.7 us (6%)
  other arithmetic  18.4 us (4%)
    psum x1, waiting for transfers between devices, local(): lax.psum((tap_grads, wide_rows, summed_loss, slot_count), ('dp', 'fsdp'))  127 us
    psum x1, blocking collectives, local(): lax.psum((tap_grads, wide_rows, summed_loss, slot_count), ('dp', 'fsdp'))  37.4 us
    all_gather x1, waiting for transfers between devices, gathered_weights(): lax.all_gather(parted[2], 'dp', axis=1, tiled=True)  29.3 us
    all_gather x1, blocking collectives, gathered_weights(): lax.all_gather(shards[1], 'fsdp', axis=0, tiled=True)  19 us
    all_gather x1, blocking collectives, gathered_weights(): lax.all_gather(shards[0], 'fsdp', axis=0, tiled=True)  17 us
    all_gather x1, blocking collectives, gathered_weights(): lax.all_gather(shards[2], 'fsdp', axis=0, tiled=True)  15.1 us
    all_gather x1, blocking collectives, gathered_weights(): lax.all_gather(shards[3], 'fsdp', axis=1, tiled=True)  13.9 us
    all_gather x1, blocking collectives, local(): lax.all_gather(lax.psum_scatter(out_grad.astype(jnp.bfloat16), 'fsdp', sc...  12.4 us
  transfers between devices with their start and end apart: 5, of which 4 were waited for; matrix products, arithmetic and copies ran while one was open for 15% of the time, Pallas kernels for 0%

profile of v1, /device:TPU:0, one launch (start us, length us, event | category | flops | bytes accessed | tf_op | source)
XLA Modules:
  0.0 414.9 jit_solution(5078676835497895429)
XLA Ops:
  8.2 17.0 %all_gather.32 = bf16[1280,160]{1,0:T(8,128)(2,1)S(1)} all-gather(bf16[160,160]{1,0:T(8,128)(2,1)S(1)} %convert_element_type.161), channel_id=1, replica_groups=mesh['dp'=4,'fsdp'=8] {'fsdp'}, dimensions={0}, use_global_device_ids=true | all-gather | bytes 460800 | tf_op jit(solution)/shard_map/all_gather | solution.py:81
  26.2 19.0 %all-gather.2 = bf16[8,400,160]{1,2,0:T(8,128)(2,1)S(1)} all-gather(bf16[1,400,160]{1,2,0:T(8,128)(2,1)S(1)} %convert_bitcast_fusion), channel_id=1, replica_groups=mesh['dp'=4,'fsdp'=8] {'fsdp'}, dimensions={0}, use_global_device_ids=true | all-gather | bytes 1152000 | tf_op jit(solution)/shard_map/all_gather | solution.py:82
  46.0 2.4 reshape.269
  48.5 15.1 %all_gather.36 = bf16[1280,160]{1,0:T(8,128)(2,1)S(1)} all-gather(bf16[160,160]{1,0:T(8,128)(2,1)S(1)} %convert_element_type.170), channel_id=1, replica_groups=mesh['dp'=4,'fsdp'=8] {'fsdp'}, dimensions={0}, use_global_device_ids=true | all-gather | bytes 460800 | tf_op jit(solution)/shard_map/all_gather | solution.py:83
  65.4 13.9 %all_gather.30 = bf16[68,320]{0,1:T(8,128)(2,1)S(1)} all-gather(bf16[68,40]{0,1:T(8,128)(2,1)S(1)} %convert_element_type.157), channel_id=1, replica_groups=mesh['dp'=4,'fsdp'=8] {'fsdp'}, dimensions={1}, use_global_device_ids=true | all-gather | bytes 48960 | tf_op jit(solution)/shard_map/all_gather | solution.py:84
  79.4 9.3 %all-gather.1 = bf16[4,320,68]{1,2,0:T(8,128)(2,1)S(1)} all-gather(bf16[1,320,68]{1,2,0:T(8,128)(2,1)S(1)} %copy.91), channel_id=1, replica_groups=mesh['dp'=4,'fsdp'=8] {'dp'}, dimensions={0}, use_global_device_ids=true | all-gather | bytes 217600 | tf_op jit(solution)/shard_map/all_gather | solution.py:90
  89.0 1.8 slice_reduce_fusion.1
  90.9 1.1 slice_reduce_fusion.6
  98.2 4.6 %convert_select_fusion = (f32[640,640]{1,0:T(8,128)}, f32[640,640]{1,0:T(8,128)}, f32[640,640]{1,0:T(8,128)S(1)}) fusion(f32[3,640,640]{2,1,0:T(8,128)} %param.35, pred[]{:T(512)} %bitcast.23, pred[]{:T(512)} %bitcast.17, pred[]{:T(512)} %bitcast.21), kind=kLoop, calls=%fused_computation.1 | loop fusion | flops 2048000 | bytes 9830403 | tf_op jit(solution)/shard_map/jit(_where)/select_n | solution.py:314
  103.1 2.2 fusion.164
  105.8 1.1 copy.112
  108.0 1.1 fusion.5
  111.2 1.1 fusion.2
  112.9 4.3 %fusion.165 = (f32[256]{0:T(256)S(1)}, f32[256,640]{1,0:T(8,128)S(1)}) fusion(f32[640]{0:T(1024)S(1)} %get-tuple-element.106, bf16[256,3200]{1,0:T(8,128)(2,1)} %fusion.2, bf16[3200,640]{0,1:T(8,128)(2,1)} %all-gather.9.cloned.1.call-done), kind=kOutput, calls=%fused_computation.312 | convolution fusion | flops 1048903424 | bytes 6393344 | tf_op jit(solution)/shard_map/dot_general | solution.py:184
  117.4 29.3 %all-gather.11.cloned.1.call-done = bf16[1280,640]{0,1:T(8,128)(2,1)} async-done(((bf16[1280,160]{0,1:T(8,128)(2,1)}), bf16[1280,640]{0,1:T(8,128)(2,1)}) %all-gather.11.cloned.1.call-update) | async-done | bytes 1638416 | tf_op jit(solution)/shard_map/all_gather | solution.py:89
  146.8 2.3 convolution_add_fusion.1
  152.7 1.5 fusion
  154.4 1.1 multiply_reduce_fusion.3
  155.5 1.1 stack.21
  156.6 1.1 stack.20
  158.8 1.1 reshape.271
  160.3 1.1 fusion.91
  161.3 4.6 %concatenate.62 = f32[64,1280]{0,1:T(8,128)} concatenate(f32[30,1280]{0,1:T(8,128)S(1)} %fusion, f32[30,1280]{0,1:T(8,128)S(1)} %fusion.150, f32[1,1280]{0,1:T(8,128)} %stack.20, f32[1,1280]{0,1:T(8,128)} %reshape.270, f32[1,1280]{0,1:T(8,128)} %reshape.271, f32[1,1280]{0,1:T(8,128)} %stack.21), dimensions={0} | concatenate | bytes 655360 | tf_op jit(solution)/shard_map/concatenate | solution.py:223
  166.6 3.4 convolution_convert_fusion
  170.0 126.9 %all-reduce.12.cloned.1.call-done = (f32[160,640]{1,0:T(8,128)}, f32[64,1280]{0,1:T(8,128)}) async-done(((f32[160,640]{1,0:T(8,128)}, f32[64,1280]{0,1:T(8,128)}), (f32[160,640]{1,0:T(8,128)}, f32[64,1280]{0,1:T(8,128)})) %all-reduce.12.cloned.1.call-update) | async-done | bytes 737296 | tf_op jit(solution)/shard_map/psum | solution.py:247
  296.9 1.5 slice.225
  298.4 2.2 slice.226
  300.6 1.4 fusion.32
  302.0 1.4 fusion.35
  306.1 1.1 stack.23
  307.2 1.1 stack.22
  309.1 2.3 fusion.55
  312.5 1.1 reshape.273
  313.6 1.1 fusion.117
  315.5 1.8 fusion.105
  320.4 1.4 fusion.153
  321.8 1.3 fusion.158
  323.1 4.3 %concatenate.65 = f32[68,1280]{0,1:T(8,128)S(1)} concatenate(f32[30,1280]{0,1:T(8,128)} %get-tuple-element.155, f32[30,1280]{0,1:T(8,128)} %get-tuple-element.154, f32[1,1280]{0,1:T(8,128)} %reshape.272, f32[1,1280]{0,1:T(8,128)} %reshape.273, f32[3,1280]{0,1:T(8,128)S(1)} %slice.225, f32[1,1280]{0,1:T(8,128)} %stack.22, f32[1,1280]{0,1:T(8,128)} %stack.23, f32[1,1280]{0,1:T(8,128)} %slice.226), dimensions={0} | concatenate | bytes 696320 | tf_op jit(solution)/shard_map/concatenate | solution.py:264
  328.2 5.6 %reduce-scatter.2.cloned.1.call-done = bf16[160,640]{1,0:T(8,128)(2,1)} async-done(((bf16[1280,640]{1,0:T(8,128)(2,1)}), bf16[160,640]{1,0:T(8,128)(2,1)}) %reduce-scatter.2.cloned.1.call-update) | async-done | bytes 204816 | tf_op jit(solution)/shard_map/reduce_scatter | solution.py:240
  333.8 12.4 %all-gather = bf16[640,640]{1,0:T(8,128)(2,1)S(1)} all-gather(bf16[160,640]{1,0:T(8,128)(2,1)} %reduce-scatter.2.cloned.1.call-done), channel_id=2, replica_groups=mesh['dp'=4,'fsdp'=8] {'dp'}, dimensions={0}, use_global_device_ids=true | all-gather | bytes 1024000 | tf_op jit(solution)/shard_map/all_gather | solution.py:239
  348.4 37.4 %all-reduce.8 = (f32[]{:T(128)}, f32[]{:T(128)}, f32[]{:T(128)}) all-reduce(f32[]{:T(128)} %get-tuple-element.126, f32[]{:T(128)} %get-tuple-element.125, f32[]{:T(128)S(6)} %add.333), channel_id=1, replica_groups=mesh['dp'=4,'fsdp'=8] {'dp','fsdp'}, use_global_device_ids=true, to_apply=%region_22.23 | all-reduce | flops 3 | bytes 24 | tf_op jit(solution)/shard_map/psum | solution.py:247
  389.9 3.1 fusion.73
  393.0 3.2 fusion.17
  396.3 2.8 fusion.170
  399.2 2.4 fusion.169
  401.6 1.4 fusion.72
  403.0 1.4 fusion.168
  404.5 1.4 fusion.151
  (196 shorter events, 27.6 us)
Async XLA Ops:
  7.2 19.0 %copy-start.25 = (f32[400,160]{0,1:T(8,128)S(1)}, f32[400,160]{0,1:T(8,128)}, u32[]{:S(2)}) copy-start(f32[400,160]{0,1:T(8,128)} %param.24) | copy-start | bytes 768004
  7.2 95.9 %all-gather.7.cloned.1.call-start = ((), (), s32[]{:S(2)}) async-start(), calls=%async_computation.1 | async-start | bytes 2048000 | tf_op jit(solution)/shard_map/all_gather | solution.py:87
  26.2 86.8 %all-gather.9.cloned.1.call-start = ((), (), s32[]{:S(2)}) async-start(), calls=%async_computation.2 | async-start | bytes 5120000 | tf_op jit(solution)/shard_map/all_gather | solution.py:88
  46.0 2.5 copy-start.27
  48.4 16.3 %copy-start.35 = (s32[2,1024]{1,0:T(2,128)S(1)}, s32[2,1024]{1,0:T(2,128)}, u32[]{:S(2)}) copy-start(s32[2,1024]{1,0:T(2,128)} %param.20) | copy-start | bytes 24580
  48.4 16.4 %copy-start.36 = (s32[2,1024]{1,0:T(2,128)S(1)}, s32[2,1024]{1,0:T(2,128)}, u32[]{:S(2)}) copy-start(s32[2,1024]{1,0:T(2,128)} %param.19) | copy-start | bytes 24580
  48.5 98.3 %all-gather.11.cloned.1.call-start = ((), (), s32[]{:S(2)}) async-start(), calls=%async_computation.3 | async-start | bytes 2048000 | tf_op jit(solution)/shard_map/all_gather | solution.py:89
  64.6 232.3 %all-reduce.12.cloned.1.call-start = ((), (), s32[]{:S(2)}) async-start(), calls=%async_computation.5 | async-start | bytes 2129920 | tf_op jit(solution)/shard_map/psum | solution.py:247
  90.8 1.7 copy-start.38
  90.8 1.7 copy-start.33
  90.8 4.4 %copy-start.37 = (s32[3]{0:T(128)S(1)}, s32[3]{0:T(128)}, u32[]{:S(2)}) copy-start(s32[3]{0:T(128)} %param.36) | copy-start | bytes 40
  98.2 4.9 %copy-start.11 = (bf16[32,1280]{0,1:T(8,128)(2,1)}, bf16[32,1280]{0,1:T(8,128)(2,1)S(1)}, u32[]{:S(2)}) copy-start(bf16[32,1280]{0,1:T(8,128)(2,1)S(1)} %fusion.52) | copy-start | bytes 245764
  105.5 1.5 copy-start.44
  105.5 1.5 copy-start.39
  117.2 31.9 %copy-start.7 = (f32[256,640]{1,0:T(8,128)}, f32[256,640]{1,0:T(8,128)S(1)}, u32[]{:S(2)}) copy-start(f32[256,640]{1,0:T(8,128)S(1)} %get-tuple-element.179) | copy-start | bytes 1966084
  149.9 0.9 copy-start.34
  152.5 1.7 copy-start.8
  152.5 1.9 copy-start.46
  152.7 2.8 copy-start.17
  165.9 167.9 %reduce-scatter.2.cloned.1.call-start = ((), (), s32[]{:S(2)}) async-start(), calls=%async_computation.4 | async-start | bytes 1843200 | tf_op jit(solution)/shard_map/reduce_scatter | solution.py:240
  296.9 3.7 copy-start.6
  296.9 6.5 %copy-start = (bf16[3200,640]{0,1:T(8,128)(2,1)S(1)}, bf16[3200,640]{0,1:T(8,128)(2,1)}, u32[]{:S(2)}) copy-start(bf16[3200,640]{0,1:T(8,128)(2,1)} %all-gather.9.cloned.1.call-done) | copy-start | bytes 12288004
  304.8 1.0 copy-start.45
  305.3 3.0 copy-start.2
  312.5 7.9 %copy-start.43 = (f32[32]{0:T(128)S(1)}, f32[32]{0:T(128)}, u32[]{:S(2)}) copy-start(f32[32]{0:T(128)} %copy-done.42) | copy-start | bytes 388
  315.5 6.2 %copy-start.1 = (f32[64,1280]{0,1:T(8,128)S(1)}, f32[64,1280]{0,1:T(8,128)}, u32[]{:S(2)}) copy-start(f32[64,1280]{0,1:T(8,128)} %get-tuple-element.131) | copy-start | bytes 983044
  317.3 1.0 copy-start.4
  327.4 0.8 copy-start.16
  327.4 62.5 %copy-start.18 = (f32[160,640]{1,0:T(8,128)S(1)}, f32[160,640]{1,0:T(8,128)}, u32[]{:S(2)}) copy-start(f32[160,640]{1,0:T(8,128)} %param.32) | copy-start | bytes 1228804
  389.9 3.1 copy-start.5
  389.9 3.1 copy-start.12
  389.9 3.1 copy-start.13
  393.0 3.3 copy-start.21
  393.0 3.3 copy-start.22
  393.0 3.2 copy-start.28
  396.2 2.9 copy-start.14
  396.2 2.9 copy-start.15
  396.3 2.8 copy-start.26
  399.1 2.4 copy-start.3
  399.1 2.4 copy-start.10
  399.1 2.4 copy-start.19
  399.1 2.4 copy-start.20
  401.6 1.4 copy-start.29
  403.0 1.5 copy-start.23
  403.0 1.5 copy-start.24
  403.0 1.5 copy-start.31
  403.0 1.5 copy-start.32
  403.0 1.5 copy-start.41
  (4 other events, 2.8 us)
Sparse Core Ops, SparseCore 0:
  26.3 32.3 all-gather.6
  61.1 51.7 all-gather.8
  115.3 31.3 all-gather.10
  166.0 130.8 all-reduce.11
  299.1 34.6 reduce-scatter.1
